TPU v7x, 32 devices: a whole 2x2x4 slice. The times are simulated.
32 devices in a mesh: row: 4 (over x, core), col: 8 (over z, y).
Axes of the slice: x: 2, y: 2, z: 4, core: 2. Of those that a mesh axis runs over, the one named last changes fastest.
Arguments:
- hamiltonian: bfloat16 [2912, 2912], P('row', 'col'), may hold values from -6 to 6
- new_atom: int32 [224], replicated, may hold values from 0 to 223, as said below
- pattern: int32 [224, 224], P('row', 'col'), may hold values 0 or 1
Outputs:
- sign_matrix: float32 [2912, 2912], P('row', 'col')
Inputs may be any that keep to these rules, and one draw needn't show every extreme that they name: `new_atom`: each old atom appears once. Block column b holds atoms b * 28 to (b + 1) * 28 - 1 in both orders. For each new block column d and each v from 0 to 27, exactly one atom of new block column d comes from old block column (d - 1 - (v mod 8)) mod 8, so the number of atoms that old block column b sends to new block column (b + k) mod 8 is the number of such v with (1 + v) mod 8 = k.
All inputs are finite; a program needn't handle non-finite values. No bound on the sum of `pattern` on one device may be relied on, other than what follows from the above.
Results may differ from a plain program's by a relative error of at most 0.0029.
Values may be sent and summed in bfloat16 or wider, within the bound.
A program may use at most 64 MiB of HBM per device.

v0:
```python
import jax
import jax.numpy as jnp
import numpy as np
from jax import lax
from jax.sharding import PartitionSpec as P

NBF = 13


def expand(atoms):
    return (atoms[:, None] * NBF + jnp.arange(NBF, dtype=jnp.int32)[None, :]).reshape(-1)


def pack_slots(new_atom, here, per_block, groups, slots):
    source = new_atom.reshape(groups, per_block) // per_block
    local = new_atom.reshape(groups, per_block) - here * per_block
    mine = source == here
    rank = jnp.cumsum(mine.astype(jnp.int32), axis=1) - 1
    number = jnp.arange(slots, dtype=jnp.int32)
    hit = mine[:, None, :] & (rank[:, None, :] == number[None, :, None])
    atoms = jnp.sum(jnp.where(hit, local[:, None, :], 0), axis=2)
    used = jnp.any(hit, axis=2)
    return (atoms.reshape(-1), jnp.repeat(used.reshape(-1), NBF))


def place_slots(new_atom, here, per_block, groups, slots):
    source = lax.dynamic_slice_in_dim(new_atom, here * per_block, per_block) // per_block
    onehot = source[:, None] == jnp.arange(groups, dtype=jnp.int32)[None, :]
    running = jnp.cumsum(onehot.astype(jnp.int32), axis=0) - 1
    rank = jnp.sum(jnp.where(onehot, running, 0), axis=1)
    return expand((source * slots + rank).astype(jnp.int32))


def fold_right(row_panel, right):
    return jnp.dot(
        row_panel,
        lax.all_gather(right, "row", axis=0, tiled=True),
        preferred_element_type=jnp.float32,
    )


def on_device(hamiltonian, new_atom, pattern):
    rows_here, cols_here = hamiltonian.shape
    row_count = lax.axis_size("row")
    col_count = lax.axis_size("col")
    order_all = rows_here * row_count
    atoms_row = rows_here // NBF
    atoms_col = cols_here // NBF
    ratio = col_count // row_count
    counts = np.bincount((1 + np.arange(atoms_col)) % col_count, minlength=col_count)
    targets = (np.arange(ratio)[:, None] + np.arange(col_count)[None, :]) % col_count // ratio
    per_target = np.sum(
        (targets[None, :, :] == np.arange(row_count)[:, None, None]) * counts[None, None, :],
        axis=(1, 2),
    )
    slots_row = max(int(np.max(per_target)), 1)
    slots_col = max(int(np.max(counts)), 1)
    row_here = lax.axis_index("row")
    col_here = lax.axis_index("col")
    atoms, flags = pack_slots(new_atom, row_here, atoms_row, row_count, slots_row)
    outgoing = jnp.where(
        flags[:, None], jnp.take(hamiltonian, expand(atoms), axis=0), jnp.zeros((), jnp.bfloat16)
    )
    arrived = lax.all_to_all(outgoing, "row", split_axis=0, concat_axis=0, tiled=True)
    moved = jnp.take(
        arrived, place_slots(new_atom, row_here, atoms_row, row_count, slots_row), axis=0
    )
    atoms, flags = pack_slots(new_atom, col_here, atoms_col, col_count, slots_col)
    outgoing = jnp.where(
        flags[None, :], jnp.take(moved, expand(atoms), axis=1), jnp.zeros((), jnp.bfloat16)
    )
    arrived = lax.all_to_all(outgoing, "col", split_axis=1, concat_axis=1, tiled=True)
    moved = jnp.take(
        arrived, place_slots(new_atom, col_here, atoms_col, col_count, slots_col), axis=1
    )
    atom_rows, atom_cols = pattern.shape
    keep = jnp.broadcast_to(
        pattern.astype(jnp.float32)[:, None, :, None], (atom_rows, NBF, atom_cols, NBF)
    ).reshape(rows_here, cols_here)
    masked = moved.astype(jnp.float32) * keep
    total = lax.psum(jnp.sum(masked * masked), ("row", "col"))
    start = (masked * lax.rsqrt(total / order_all)).astype(jnp.bfloat16)
    first = lax.all_gather(start, "col", axis=1, tiled=True)
    square = (fold_right(first, start) * keep).astype(jnp.bfloat16)
    second = lax.all_gather(start, "col", axis=1, tiled=True)
    cube = fold_right(second, square) * keep
    return keep * (1.5 * start.astype(jnp.float32) - 0.5 * cube)


def solution(mesh):
    in_specs = (P("row", "col"), P(), P("row", "col"))
    out_specs = P("row", "col")
    return jax.shard_map(
        on_device, mesh=mesh, in_specs=in_specs, out_specs=out_specs, check_vma=False
    )
```

profile of v0, /device:TPU:0, one launch (start us, length us, event | category | flops | bytes accessed | tf_op | source)
XLA Modules:
  0.0 246.0 jit_solution(5118682109715307969)
XLA Ops:
  6.5 0.8 compare_and_fusion.5
  7.3 0.7 broadcast_divide_fusion.1
  8.0 0.1 sub.80
  8.1 0.1 and.101
  8.2 0.1 div.54
  8.3 0.2 reduce_window_sum.47
  8.5 0.2 fusion.9
  8.6 0.2 select_reduce_fusion
  8.8 0.1 mul.113
  9.0 0.2 add.307
  9.2 0.1 add.298
  9.3 0.1 add.300
  9.5 0.1 broadcast_in_dim.144
  9.6 3.5 %gather_fusion = bf16[832,364]{1,0:T(8,128)(2,1)S(1)} fusion(bf16[728,364]{1,0:T(8,128)(2,1)S(1)} %copy-done, s32[1024]{0:T(1024)S(1)} %pad_clamp_fusion.3), kind=kCustom, calls=%fused_computation | custom fusion | bytes 1214720 | tf_op jit(solution)/shard_map/jit(_take)/gather | solution.py:62
  13.2 1.1 select_select_fusion.1
  14.3 4.2 %all-to-all-start = ((bf16[4,208,364]{2,1,0:T(8,128)(2,1)}), bf16[4,208,364]{2,1,0:T(8,128)(2,1)S(1)}, u32[]{:S(2)}, u32[]{:S(2)}) async-start(bf16[4,208,364]{2,1,0:T(8,128)(2,1)} %select_select_fusion.1), calls=%async_computation | async-start | bytes 1277952 | tf_op jit(solution)/shard_map/all_to_all | solution.py:64
  18.5 0.1 and_select_fusion
  18.7 0.1 reduce_window_sum.46
  18.8 0.2 select_reduce_fusion.1
  19.0 0.1 add_multiply_fusion
  19.1 0.1 add.310
  19.4 0.1 and.94
  19.6 0.2 reduce_window_sum.45
  19.8 0.1 fusion.13
  19.9 0.2 select_reduce_fusion.2
  20.1 0.1 copy.26
  20.3 0.1 add.316
  20.5 0.1 and_select_fusion.1
  20.5 0.1 add.294
  20.7 0.1 add.283
  20.9 0.1 copy.25
  21.1 0.1 broadcast_in_dim.136
  21.2 7.4 %all-to-all-done = bf16[4,208,364]{2,1,0:T(8,128)(2,1)S(1)} async-done(((bf16[4,208,364]{2,1,0:T(8,128)(2,1)}), bf16[4,208,364]{2,1,0:T(8,128)(2,1)S(1)}, u32[]{:S(2)}, u32[]{:S(2)}) %all-to-all-start) | async-done | bytes 605728 | tf_op jit(solution)/shard_map/all_to_all | solution.py:64
  28.6 3.0 %gather_fusion.1 = bf16[728,364]{1,0:T(8,128)(2,1)S(1)} fusion(bf16[832,364]{1,0:T(8,128)(2,1)S(1)} %bitcast.33, s32[1024]{0:T(1024)S(1)} %pad_clamp_fusion.2), kind=kCustom, calls=%fused_computation.1 | custom fusion | bytes 1062880 | tf_op jit(solution)/shard_map/jit(_take)/gather | solution.py:65
  31.5 0.2 broadcast_select_fusion
  31.7 0.2 copy.28
  32.0 2.2 gather_fusion.2
  34.1 0.1 gather.24
  34.3 1.0 select_select_fusion
  35.3 6.5 %all-to-all-start.1 = ((bf16[728,8,52]{0,2,1:T(8,128)(2,1)}), bf16[728,8,52]{0,2,1:T(8,128)(2,1)S(1)}, u32[]{:S(2)}, u32[]{:S(2)}) async-start(bf16[728,8,52]{0,2,1:T(8,128)(2,1)} %select_select_fusion), calls=%async_computation.1 | async-start | bytes 1376256 | tf_op jit(solution)/shard_map/all_to_all | solution.py:72
  42.0 0.2 select_reduce_fusion.3
  42.2 0.1 add_multiply_fusion.1
  42.4 0.1 add.319
  42.5 0.1 add.279
  42.6 4.7 %broadcast_in_dim.132 = f32[56,13,28,13]{1,0,3,2:T(8,128)} broadcast(f32[56,28]{0,1:T(8,128)S(1)} %convert_element_type.41), dimensions={0,2} | broadcast | bytes 1066240 | tf_op jit(solution)/shard_map/broadcast_in_dim | solution.py:77
  47.3 6.7 %reshape.368 = f32[728,364]{0,1:T(8,128)S(1)} reshape(f32[56,13,28,13]{1,0,3,2:T(8,128)} %broadcast_in_dim.132) | data formatting | bytes 2119936 | tf_op jit(solution)/shard_map/reshape | solution.py:79
  54.1 0.4 copy.36
  54.5 0.1 broadcast_in_dim.154
  54.7 4.9 %all-to-all-done.1 = bf16[728,8,52]{0,2,1:T(8,128)(2,1)S(1)} async-done(((bf16[728,8,52]{0,2,1:T(8,128)(2,1)}), bf16[728,8,52]{0,2,1:T(8,128)(2,1)S(1)}, u32[]{:S(2)}, u32[]{:S(2)}) %all-to-all-start.1) | async-done | bytes 605728 | tf_op jit(solution)/shard_map/all_to_all | solution.py:72
  59.6 0.3 all_to_all.15
  59.8 2.2 gather_fusion.3
  62.0 0.3 copy.29
  62.3 0.9 fusion.5
  63.2 38.4 %psum.7 = f32[]{:T(128)} all-reduce(f32[]{:T(128)} %fusion.5), channel_id=1, replica_groups=mesh['row'=4,'col'=8] {'row','col'}, use_global_device_ids=true, to_apply=%region_11.12 | all-reduce | flops 1 | bytes 8 | tf_op jit(solution)/shard_map/psum | solution.py:81
  102.3 1.0 fusion.7
  103.3 0.7 all-gather.5.cloned.1.call-update
  104.1 0.2 all-gather.7.cloned.1.call-start
  104.3 75.6 %all-gather.9.cloned.1.call-done = bf16[8,364,728]{1,2,0:T(8,128)(2,1)} async-done(((bf16[1,364,728]{1,2,0:T(8,128)(2,1)}), bf16[8,364,728]{1,2,0:T(8,128)(2,1)}) %all-gather.9.cloned.1.call-update) | async-done | bytes 4239888 | tf_op jit(solution)/shard_map/all_gather | solution.py:85
  179.9 4.9 %copy.33 = bf16[8,364,728]{1,0,2:T(8,128)(2,1)} copy(bf16[8,364,728]{1,2,0:T(8,128)(2,1)} %all-gather.9.cloned.1.call-done) | data formatting | bytes 8479744 | tf_op jit(solution)/shard_map/all_gather | solution.py:85
  184.8 8.7 %reshape.402 = bf16[2912,728]{0,1:T(8,128)(2,1)} reshape(bf16[8,364,728]{1,0,2:T(8,128)(2,1)} %copy.33) | data formatting | bytes 8479744
  193.5 9.8 %all-gather.5.cloned.1.call-done = bf16[2912,364]{1,0:T(8,128)(2,1)} async-done(((bf16[728,364]{1,0:T(8,128)(2,1)}), bf16[2912,364]{1,0:T(8,128)(2,1)}) %all-gather.5.cloned.1.call-update) | async-done | bytes 2119952 | tf_op jit(solution)/shard_map/all_gather | solution.py:37
  203.3 6.2 %fusion.3 = bf16[728,364]{1,0:T(8,128)(2,1)} fusion(f32[728,364]{1,0:T(8,128)S(1)} %copy.36, bf16[2912,728]{0,1:T(8,128)(2,1)} %reshape.402, bf16[2912,364]{1,0:T(8,128)(2,1)} %all-gather.5.cloned.1.call-done), kind=kOutput, calls=%fused_computation.9 | convolution fusion | flops 1543843328 | bytes 7949760 | tf_op jit(solution)/shard_map/dot_general | solution.py:35
  209.5 23.5 %all-gather.7.cloned.1.call-done = bf16[2912,364]{1,0:T(8,128)(2,1)} async-done(((bf16[728,364]{1,0:T(8,128)(2,1)}), bf16[2912,364]{1,0:T(8,128)(2,1)}) %all-gather.7.cloned.1.call-update) | async-done | bytes 2119952 | tf_op jit(solution)/shard_map/all_gather | solution.py:37
  233.0 6.4 %fusion.2 = f32[728,364]{1,0:T(8,128)} fusion(f32[728,364]{1,0:T(8,128)S(1)} %copy.36, bf16[2912,728]{0,1:T(8,128)(2,1)} %reshape.402, bf16[2912,364]{1,0:T(8,128)(2,1)} %all-gather.7.cloned.1.call-done, bf16[728,364]{1,0:T(8,128)(2,1)S(1)} %copy-done.1), kind=kOutput, calls=%fused_computation.8 | convolution fusion | flops 1544903168 | bytes 9009728 | tf_op jit(solution)/shard_map/dot_general | solution.py:35
  (49 shorter events, 1.5 us)
Async XLA Ops:
  6.5 3.1 %copy-start = (bf16[728,364]{1,0:T(8,128)(2,1)S(1)}, bf16[728,364]{1,0:T(8,128)(2,1)}, u32[]{:S(2)}) copy-start(bf16[728,364]{1,0:T(8,128)(2,1)} %param.3) | copy-start | bytes 1589956
  13.1 5.4 %copy-start.3 = (s32[224]{0:T(256)S(1)}, s32[224]{0:T(256)}, u32[]{:S(2)}) copy-start(s32[224]{0:T(256)} %param.4) | copy-start | bytes 2692
  14.3 14.3 %all-to-all-start = ((bf16[4,208,364]{2,1,0:T(8,128)(2,1)}), bf16[4,208,364]{2,1,0:T(8,128)(2,1)S(1)}, u32[]{:S(2)}, u32[]{:S(2)}) async-start(bf16[4,208,364]{2,1,0:T(8,128)(2,1)} %select_select_fusion.1), calls=%async_computation | async-start | bytes 1277952 | tf_op jit(solution)/shard_map/all_to_all | solution.py:64
  34.3 8.3 %copy-start.2 = (s32[56,28]{0,1:T(8,128)S(1)}, s32[56,28]{0,1:T(8,128)}, u32[]{:S(2)}) copy-start(s32[56,28]{0,1:T(8,128)} %param.5) | copy-start | bytes 18820
  35.3 24.2 %all-to-all-start.1 = ((bf16[728,8,52]{0,2,1:T(8,128)(2,1)}), bf16[728,8,52]{0,2,1:T(8,128)(2,1)S(1)}, u32[]{:S(2)}, u32[]{:S(2)}) async-start(bf16[728,8,52]{0,2,1:T(8,128)(2,1)} %select_select_fusion), calls=%async_computation.1 | async-start | bytes 1376256 | tf_op jit(solution)/shard_map/all_to_all | solution.py:72
  41.9 138.0 %all-gather.9.cloned.1.call-start = ((), (), s32[]{:S(2)}) async-start(), calls=%async_computation.4 | async-start | bytes 5031936 | tf_op jit(solution)/shard_map/all_gather | solution.py:85
  103.3 100.0 %all-gather.5.cloned.1.call-start = ((), (), s32[]{:S(2)}) async-start(), calls=%async_computation.2 | async-start | bytes 2795520 | tf_op jit(solution)/shard_map/all_gather | solution.py:37
  104.1 129.0 %all-gather.7.cloned.1.call-start = ((), (), s32[]{:S(2)}) async-start(), calls=%async_computation.3 | async-start | bytes 2795520 | tf_op jit(solution)/shard_map/all_gather | solution.py:37
  193.5 39.5 %copy-start.1 = (bf16[728,364]{1,0:T(8,128)(2,1)S(1)}, bf16[728,364]{1,0:T(8,128)(2,1)}, u32[]{:S(2)}) copy-start(bf16[728,364]{1,0:T(8,128)(2,1)} %fusion.7) | copy-start | bytes 1589956
Sparse Core Ops, SparseCore 0:
  103.4 76.4 all-gather.8
  181.4 21.7 all-gather.4
  209.7 23.3 all-gather.6
where the time goes:
time: 247 us; the launch traced here: 246 us
  waiting for transfers between devices  122 us (49%)
  local copies, waits for them, and re-layouts  39.7 us (16%)
  blocking collectives  38.4 us (16%)
  between operations  14.1 us (6%)
  matrix products  12.7 us (5%)
  starting transfers between devices  11.1 us (4%)
  other arithmetic  8.25 us (3%)
    all_gather x1, waiting for transfers between devices, on_device(): second = lax.all_gather(start, 'col', axis=1, tiled=True)  75.6 us
    psum x1, blocking collectives, on_device(): total = lax.psum(jnp.sum(masked * masked), ('row', 'col'))  38.4 us
    all_gather x2, waiting for transfers between devices, fold_right(): lax.all_gather(right, 'row', axis=0, tiled=True)  33.3 us
    dot_general x2, matrix products, fold_right(): jnp.dot(row_panel, lax.all_gather(right, 'row', axis=0, tiled=True), pref...  12.7 us
    unnamed x9, local copies, waits for them, and re-layouts  8.69 us
    all_to_all x1, waiting for transfers between devices, on_device(): lax.all_to_all(outgoing, 'row', split_axis=0, concat_axis=0, tiled=True)  7.35 us
    reshape x2, local copies, waits for them, and re-layouts, on_device(): keep = jnp.broadcast_to(pattern.astype(jnp.float32)[:, None, :, None], (a...  7.1 us
    all_to_all x1, starting transfers between devices, on_device(): lax.all_to_all(outgoing, 'col', split_axis=1, concat_axis=1, tiled=True)  6.53 us
  transfers between devices with their start and end apart: 5, of which 5 were waited for; matrix products, arithmetic and copies ran while one was open for 12% of the time, Pallas kernels for 0%

commit v1 on v0

--- a/solution.py
+++ b/solution.py
@@ -82,7 +82,7 @@
     start = (masked * lax.rsqrt(total / order_all)).astype(jnp.bfloat16)
     first = lax.all_gather(start, "col", axis=1, tiled=True)
     square = (fold_right(first, start) * keep).astype(jnp.bfloat16)
-    second = lax.all_gather(start, "col", axis=1, tiled=True)
+    second = jnp.concatenate(lax.all_gather(start, "col"), axis=1)
     cube = fold_right(second, square) * keep
     return keep * (1.5 * start.astype(jnp.float32) - 0.5 * cube)
 

time: 247 us -> 319 us (1.29)
  waiting for transfers between devices: 122 us -> 170 us
  local copies, waits for them, and re-layouts: 39.7 us -> 61.5 us
    all_gather x1 -> x2, waiting for transfers between devices: 75.6 us -> 137 us  [the longest x1 72.3 us: on_device(): second = jnp.concatenate(lax.all_gather(start, 'col'), axis=1)]
    all_gather x2, waiting for transfers between devices: 33.3 us -> 19.3 us  [fold_right(): lax.all_gather(right, 'row', axis=0, tiled=True)]
    reshape x0 -> x2, local copies, waits for them, and re-layouts: none -> 13.7 us  [on_device(): second = jnp.concatenate(lax.all_gather(start, 'col'), axis=1)]
    reshape x2 -> x4, local copies, waits for them, and re-layouts: 7.1 us -> 15.2 us  [on_device(): keep = jnp.broadcast_to(pattern.astype(jnp.float32)[:, None, :, None], (a...]
  transfers between devices with their start and end apart: 5 -> 6, of which waited for: 5 -> 6; matrix products, arithmetic and copies ran while one was open for 12% -> 19% of each run, Pallas kernels for 0% -> 0%
where the time goes in v1:
time: 319 us; the launch traced here: 318 us
  waiting for transfers between devices  170 us (53%)
  local copies, waits for them, and re-layouts  61.5 us (19%)
  blocking collectives  38.4 us (12%)
  between operations  14.1 us (4%)
  matrix products  12.7 us (4%)
  starting transfers between devices  11.1 us (3%)
  other arithmetic  10.6 us (3%)
    all_gather x1, waiting for transfers between devices, on_device(): second = jnp.concatenate(lax.all_gather(start, 'col'), axis=1)  72.3 us
    all_gather x1, waiting for transfers between devices, on_device(): first = lax.all_gather(start, 'col', axis=1, tiled=True)  65 us
    psum x1, blocking collectives, on_device(): total = lax.psum(jnp.sum(masked * masked), ('row', 'col'))  38.4 us
    all_gather x2, waiting for transfers between devices, fold_right(): lax.all_gather(right, 'row', axis=0, tiled=True)  19.3 us
    reshape x4, local copies, waits for them, and re-layouts, on_device(): keep = jnp.broadcast_to(pattern.astype(jnp.float32)[:, None, :, None], (a...  15.2 us
    reshape x2, local copies, waits for them, and re-layouts, on_device(): second = jnp.concatenate(lax.all_gather(start, 'col'), axis=1)  13.7 us
    dot_general x2, matrix products, fold_right(): jnp.dot(row_panel, lax.all_gather(right, 'row', axis=0, tiled=True), pref...  12.7 us
    unnamed x9, local copies, waits for them, and re-layouts  8.7 us
  transfers between devices with their start and end apart: 6, of which 6 were waited for; matrix products, arithmetic and copies ran while one was open for 19% of the time, Pallas kernels for 0%

profile of v1, /device:TPU:0, one launch (start us, length us, event | category | flops | bytes accessed | tf_op | source)
XLA Modules:
  0.0 318.0 jit_solution(3479221268036356339)
XLA Ops:
  6.5 0.8 compare_and_fusion.5
  7.3 0.1 and.101
  7.4 0.7 broadcast_divide_fusion.1
  8.2 0.2 reduce_window_sum.47
  8.5 0.1 fusion.5
  8.6 0.2 select_reduce_fusion
  9.0 0.1 broadcast_in_dim.148
  9.1 0.1 add.298
  9.3 0.1 add.307
  9.5 0.1 add.300
  9.6 3.5 %gather_fusion = bf16[832,364]{1,0:T(8,128)(2,1)S(1)} fusion(bf16[728,364]{1,0:T(8,128)(2,1)S(1)} %copy-done, s32[1024]{0:T(1024)S(1)} %pad_clamp_fusion.3), kind=kCustom, calls=%fused_computation | custom fusion | bytes 1214720 | tf_op jit(solution)/shard_map/jit(_take)/gather | solution.py:62
  13.1 1.1 select_select_fusion.1
  14.3 4.2 %all-to-all-start = ((bf16[4,208,364]{2,1,0:T(8,128)(2,1)}), bf16[4,208,364]{2,1,0:T(8,128)(2,1)S(1)}, u32[]{:S(2)}, u32[]{:S(2)}) async-start(bf16[4,208,364]{2,1,0:T(8,128)(2,1)} %select_select_fusion.1), calls=%async_computation | async-start | bytes 1277952 | tf_op jit(solution)/shard_map/all_to_all | solution.py:64
  18.6 0.1 and.94
  18.8 0.2 reduce_window_sum.45
  19.0 0.1 fusion.9
  19.2 0.2 select_reduce_fusion.2
  19.6 0.1 add.316
  19.8 0.1 reduce_window_sum.46
  19.9 0.2 select_reduce_fusion.1
  20.1 0.1 add_multiply_fusion
  20.3 0.1 add.310
  20.4 0.1 and_select_fusion.1
  20.5 0.1 add.294
  20.7 0.1 copy.26
  20.8 0.1 broadcast_in_dim.140
  21.2 7.4 %all-to-all-done = bf16[4,208,364]{2,1,0:T(8,128)(2,1)S(1)} async-done(((bf16[4,208,364]{2,1,0:T(8,128)(2,1)}), bf16[4,208,364]{2,1,0:T(8,128)(2,1)S(1)}, u32[]{:S(2)}, u32[]{:S(2)}) %all-to-all-start) | async-done | bytes 605728 | tf_op jit(solution)/shard_map/all_to_all | solution.py:64
  28.6 3.0 gather_fusion.1
  31.5 0.2 broadcast_select_fusion
  31.7 0.2 copy.29
  31.9 2.2 gather_fusion.2
  34.1 0.1 gather.26
  34.3 1.0 select_select_fusion
  35.3 6.5 %all-to-all-start.1 = ((bf16[728,8,52]{0,2,1:T(8,128)(2,1)}), bf16[728,8,52]{0,2,1:T(8,128)(2,1)S(1)}, u32[]{:S(2)}, u32[]{:S(2)}) async-start(bf16[728,8,52]{0,2,1:T(8,128)(2,1)} %select_select_fusion), calls=%async_computation.1 | async-start | bytes 1376256 | tf_op jit(solution)/shard_map/all_to_all | solution.py:72
  42.0 0.2 select_reduce_fusion.3
  42.2 0.1 add_multiply_fusion.1
  42.4 0.1 add.319
  42.5 0.1 add.279
  42.7 0.1 broadcast_in_dim.158
  42.8 4.7 %broadcast_in_dim.136 = f32[56,13,28,13]{1,0,3,2:T(8,128)} broadcast(f32[56,28]{0,1:T(8,128)S(1)} %convert_element_type.59), dimensions={0,2} | broadcast | bytes 1066240 | tf_op jit(solution)/shard_map/broadcast_in_dim | solution.py:77
  47.5 6.7 %reshape.422 = f32[728,364]{0,1:T(8,128)S(1)} reshape(f32[56,13,28,13]{1,0,3,2:T(8,128)} %broadcast_in_dim.136) | data formatting | bytes 2119936 | tf_op jit(solution)/shard_map/reshape | solution.py:79
  54.3 0.4 copy.38
  54.7 4.9 %all-to-all-done.1 = bf16[728,8,52]{0,2,1:T(8,128)(2,1)S(1)} async-done(((bf16[728,8,52]{0,2,1:T(8,128)(2,1)}), bf16[728,8,52]{0,2,1:T(8,128)(2,1)S(1)}, u32[]{:S(2)}, u32[]{:S(2)}) %all-to-all-start.1) | async-done | bytes 605728 | tf_op jit(solution)/shard_map/all_to_all | solution.py:72
  59.6 0.3 all_to_all.15
  59.8 2.2 gather_fusion.3
  62.0 0.3 copy.30
  62.3 0.9 multiply_reduce_fusion
  63.2 38.4 %psum.7 = f32[]{:T(128)} all-reduce(f32[]{:T(128)} %multiply_reduce_fusion), channel_id=1, replica_groups=mesh['row'=4,'col'=8] {'row','col'}, use_global_device_ids=true, to_apply=%region_11.12 | all-reduce | flops 1 | bytes 8 | tf_op jit(solution)/shard_map/psum | solution.py:81
  102.3 1.0 multiply_convert_fusion.1
  103.4 0.7 all-gather.8.cloned.1.call-update
  104.1 6.8 %reshape.423 = f32[1,728,364]{1,2,0:T(8,128)S(1)} reshape(f32[56,13,28,13]{1,0,3,2:T(8,128)} %broadcast_in_dim.136) | data formatting | bytes 2119936 | tf_op jit(solution)/shard_map/reshape | solution.py:79
  110.9 1.4 copy.33
  112.2 2.4 multiply_convert_fusion
  114.6 0.2 all-gather.10.cloned.1.call-start
  114.9 65.0 %all-gather.12.cloned.1.call-done = bf16[8,364,728]{1,2,0:T(8,128)(2,1)} async-done(((bf16[1,364,728]{1,2,0:T(8,128)(2,1)}), bf16[8,364,728]{1,2,0:T(8,128)(2,1)}) %all-gather.12.cloned.1.call-update) | async-done | bytes 4239888 | tf_op jit(solution)/shard_map/all_gather | solution.py:83
  179.9 4.9 %copy.35 = bf16[8,364,728]{1,0,2:T(8,128)(2,1)} copy(bf16[8,364,728]{1,2,0:T(8,128)(2,1)} %all-gather.12.cloned.1.call-done) | data formatting | bytes 8479744 | tf_op jit(solution)/shard_map/all_gather | solution.py:83
  184.9 8.7 %reshape.459 = bf16[2912,728]{0,1:T(8,128)(2,1)} reshape(bf16[8,364,728]{1,0,2:T(8,128)(2,1)} %copy.35) | data formatting | bytes 8479744
  193.5 9.8 %all-gather.8.cloned.1.call-done = bf16[2912,364]{1,0:T(8,128)(2,1)} async-done(((bf16[728,364]{1,0:T(8,128)(2,1)}), bf16[2912,364]{1,0:T(8,128)(2,1)}) %all-gather.8.cloned.1.call-update) | async-done | bytes 2119952 | tf_op jit(solution)/shard_map/all_gather | solution.py:37
  203.3 6.2 %fusion.3 = bf16[728,364]{1,0:T(8,128)(2,1)} fusion(f32[728,364]{1,0:T(8,128)S(1)} %copy.38, bf16[2912,728]{0,1:T(8,128)(2,1)} %reshape.459, bf16[2912,364]{1,0:T(8,128)(2,1)} %all-gather.8.cloned.1.call-done), kind=kOutput, calls=%fused_computation.9 | convolution fusion | flops 1543843328 | bytes 7949760 | tf_op jit(solution)/shard_map/dot_general | solution.py:35
  209.5 72.3 %all-gather.6.cloned.1.call-done = bf16[8,728,364]{2,1,0:T(8,128)(2,1)} async-done(((bf16[1,728,364]{2,1,0:T(8,128)(2,1)}), bf16[8,728,364]{2,1,0:T(8,128)(2,1)}) %all-gather.6.cloned.1.call-update) | async-done | bytes 4239888 | tf_op jit(solution)/shard_map/all_gather | solution.py:85
  281.8 4.9 %copy.34 = bf16[728,8,364]{2,1,0:T(8,128)(2,1)} copy(bf16[728,8,364]{2,0,1:T(8,128)(2,1)} %bitcast.40) | data formatting | bytes 8479744 | tf_op jit(solution)/shard_map/reshape | solution.py:85
  286.7 8.7 %reshape.425 = bf16[728,2912]{1,0:T(8,128)(2,1)} reshape(bf16[728,8,364]{2,1,0:T(8,128)(2,1)} %copy.34) | data formatting | bytes 8479744 | tf_op jit(solution)/shard_map/reshape | solution.py:85
  295.5 9.5 %all-gather.10.cloned.1.call-done = bf16[2912,364]{1,0:T(8,128)(2,1)} async-done(((bf16[728,364]{1,0:T(8,128)(2,1)}), bf16[2912,364]{1,0:T(8,128)(2,1)}) %all-gather.10.cloned.1.call-update) | async-done | bytes 2119952 | tf_op jit(solution)/shard_map/all_gather | solution.py:37
  305.0 6.4 %fusion.2 = f32[728,364]{1,0:T(8,128)} fusion(f32[728,364]{1,0:T(8,128)S(1)} %copy.38, bf16[728,2912]{1,0:T(8,128)(2,1)} %reshape.425, bf16[2912,364]{1,0:T(8,128)(2,1)} %all-gather.10.cloned.1.call-done, bf16[728,364]{1,0:T(8,128)(2,1)S(1)} %copy-done.1), kind=kOutput, calls=%fused_computation.8 | convolution fusion | flops 1544903168 | bytes 9009728 | tf_op jit(solution)/shard_map/dot_general | solution.py:35
  (57 shorter events, 2.0 us)
Async XLA Ops:
  6.5 3.1 copy-start
  13.1 5.4 %copy-start.3 = (s32[224]{0:T(256)S(1)}, s32[224]{0:T(256)}, u32[]{:S(2)}) copy-start(s32[224]{0:T(256)} %param.4) | copy-start | bytes 2692
  14.3 14.3 %all-to-all-start = ((bf16[4,208,364]{2,1,0:T(8,128)(2,1)}), bf16[4,208,364]{2,1,0:T(8,128)(2,1)S(1)}, u32[]{:S(2)}, u32[]{:S(2)}) async-start(bf16[4,208,364]{2,1,0:T(8,128)(2,1)} %select_select_fusion.1), calls=%async_computation | async-start | bytes 1277952 | tf_op jit(solution)/shard_map/all_to_all | solution.py:64
  34.3 8.5 %copy-start.2 = (s32[56,28]{0,1:T(8,128)S(1)}, s32[56,28]{0,1:T(8,128)}, u32[]{:S(2)}) copy-start(s32[56,28]{0,1:T(8,128)} %param.5) | copy-start | bytes 18820
  35.3 24.2 %all-to-all-start.1 = ((bf16[728,8,52]{0,2,1:T(8,128)(2,1)}), bf16[728,8,52]{0,2,1:T(8,128)(2,1)S(1)}, u32[]{:S(2)}, u32[]{:S(2)}) async-start(bf16[728,8,52]{0,2,1:T(8,128)(2,1)} %select_select_fusion), calls=%async_computation.1 | async-start | bytes 1376256 | tf_op jit(solution)/shard_map/all_to_all | solution.py:72
  41.9 138.0 %all-gather.12.cloned.1.call-start = ((), (), s32[]{:S(2)}) async-start(), calls=%async_computation.5 | async-start | bytes 5031936 | tf_op jit(solution)/shard_map/all_gather | solution.py:83
  103.3 100.0 %all-gather.8.cloned.1.call-start = ((), (), s32[]{:S(2)}) async-start(), calls=%async_computation.3 | async-start | bytes 2795520 | tf_op jit(solution)/shard_map/all_gather | solution.py:37
  104.1 177.7 %all-gather.6.cloned.1.call-start = ((), (), s32[]{:S(2)}) async-start(), calls=%async_computation.2 | async-start | bytes 5031936 | tf_op jit(solution)/shard_map/all_gather | solution.py:85
  114.6 190.4 %all-gather.10.cloned.1.call-start = ((), (), s32[]{:S(2)}) async-start(), calls=%async_computation.4 | async-start | bytes 2795520 | tf_op jit(solution)/shard_map/all_gather | solution.py:37
  286.7 18.3 %copy-start.1 = (bf16[728,364]{1,0:T(8,128)(2,1)S(1)}, bf16[728,364]{1,0:T(8,128)(2,1)}, u32[]{:S(2)}) copy-start(bf16[728,364]{1,0:T(8,128)(2,1)} %multiply_convert_fusion.1) | copy-start | bytes 1589956
Sparse Core Ops, SparseCore 0:
  103.4 76.4 all-gather.11
  181.5 21.7 all-gather.7
  205.5 76.2 all-gather.5
  283.2 21.7 all-gather.9
